TPU v7x, 256 devices: a 8x8x2 block of a 8x8x16 slice. The times are simulated.
256 devices in a mesh: groups: 2 (over z), seq: 16 (over y, core), dp: 8 (over x).
Axes of the slice: x: 8, y: 8, z: 2, core: 2. Of those that a mesh axis runs over, the one named last changes fastest.
The devices are a block of a 8x8x16 slice.
Arguments:
- resid: bfloat16 [16, 1024, 2048], P(('groups', 'dp'), 'seq'), parts along dimension 0, may hold values from -6 to 6
- queries_keys: bfloat16 [2, 16, 1024, 2048], P(None, ('groups', 'dp'), 'seq'), parts along dimension 1, may hold values from -20 to 20
- values: bfloat16 [16, 1024, 2048], P(('groups', 'dp'), 'seq'), parts along dimension 0, may hold values from -6 to 6
- doc_ids: int32 [16, 1024], P(('groups', 'dp')), parts along dimension 0, may hold values from 0 to 5, never falling along the last dimension, each value on 1 to 512 neighbouring positions
- out_weight: bfloat16 [2048, 2048], P(None, 'dp'), may hold values from -0.125 to 0.125
- norm_gain: float32 [2048], replicated, may hold values from 0.5 to 1.5
- expert_ids: int32 [16, 1024, 4], P(('groups', 'dp'), 'seq'), parts along dimension 0, may hold values from 0 to 31, all different within a row; in each aligned block of 64 rows (0 to 63, 64 to 127, ..., all dimensions but the last counted through in order) at most 10 rows name the same one
- gate_vals: float32 [16, 1024, 4], P(('groups', 'dp'), 'seq'), parts along dimension 0, may hold values from 0.05 to 0.6
- expert_gate: bfloat16 [128, 2048, 352], P(('seq', 'dp')), may hold values from -0.125 to 0.125
- expert_up: bfloat16 [128, 2048, 352], P(('seq', 'dp')), may hold values from -0.125 to 0.125
- expert_down: bfloat16 [128, 352, 2048], P(('seq', 'dp')), may hold values from -0.15625 to 0.15625
- shared_gate: bfloat16 [2048, 2816], P(None, 'dp'), may hold values from -0.125 to 0.125
- shared_up: bfloat16 [2048, 2816], P(None, 'dp'), may hold values from -0.125 to 0.125
- shared_down: bfloat16 [2816, 2048], P('dp'), may hold values from -0.109375 to 0.109375
- shared_score: bfloat16 [2048], replicated, may hold values from -0.125 to 0.125
Outputs:
- layer_out: bfloat16 [16, 1024, 2048], P(('groups', 'dp'), 'seq'), parts along dimension 0
There are 2 independent parts, one for each index of `groups`. A program takes and returns all parts, laid end to end along the dimension named above; an argument that names none is the same for every part. Nothing has to cross between parts.
Inputs may be any that keep to these rules, and one draw needn't show every extreme that they name: `doc_ids`: document numbers never fall along a sequence; each document holds 1 to 512 positions. `expert_ids`: each token names 4 different experts; among the rows of one device no expert is named more than 10 times.
All inputs are finite; a program needn't handle non-finite values.
Results may differ from a plain program's by a relative error of at most 0.01.
Values may be sent and summed in bfloat16 or wider, within the bound.
A program may use at most 128 MiB of HBM per device.

v0:
```python
import math
import jax
import jax.numpy as jnp
from jax import lax
from jax.sharding import PartitionSpec as P

HD = 128
EXPERTS = 32
TOPK = 4
SPLIT = 4
CAP = 10
norm_eps = 1e-06


def slot_numbers(routes):
    flat_routes = routes.reshape(routes.shape[:-2] + (-1,))
    matches = (flat_routes[..., None] == jnp.arange(EXPERTS, dtype=jnp.int32)).astype(jnp.int32)
    ranked = jnp.sum(matches * (jnp.cumsum(matches, axis=-2) - 1), axis=-1)
    return (flat_routes * CAP + ranked).reshape(routes.shape)


def attend_heads(queries, key_rows, value_rows, documents):
    score_scale = 1.0 / math.sqrt(queries.shape[-1])
    scores = (
        jnp.einsum("qhd,khd->hqk", queries, key_rows, preferred_element_type=jnp.float32)
        * score_scale
    )
    positions = jnp.arange(queries.shape[0], dtype=jnp.int32)
    allowed = (positions[:, None] >= positions[None, :]) & (
        documents[:, None] == documents[None, :]
    )
    scores = jnp.where(allowed[None], scores, -1e30)
    row_max = jnp.max(scores, axis=-1, keepdims=True)
    lifted = jnp.exp(scores - row_max)
    weights = (lifted / jnp.sum(lifted, axis=-1, keepdims=True)).astype(jnp.bfloat16)
    return jnp.einsum(
        "hqk,khd->qhd", weights, value_rows, preferred_element_type=jnp.float32
    ).astype(jnp.bfloat16)


def piece_block(row_block, gate_matrix, up_matrix, down_matrix):
    gate_act = jnp.einsum(
        "npcd,pdf->npcf", row_block, gate_matrix, preferred_element_type=jnp.float32
    )
    up_act = jnp.einsum("npcd,pdf->npcf", row_block, up_matrix, preferred_element_type=jnp.float32)
    hidden = (jax.nn.silu(gate_act) * up_act).astype(jnp.bfloat16)
    return jnp.einsum(
        "npcf,pfd->npcd", hidden, down_matrix, preferred_element_type=jnp.float32
    ).astype(jnp.bfloat16)


def shared_block(row_block, gate_matrix, up_matrix, down_matrix):
    gate_act = jnp.dot(row_block, gate_matrix, preferred_element_type=jnp.float32)
    up_act = jnp.dot(row_block, up_matrix, preferred_element_type=jnp.float32)
    hidden = (jax.nn.silu(gate_act) * up_act).astype(jnp.bfloat16)
    return jnp.dot(hidden, down_matrix, preferred_element_type=jnp.float32)


def body(
    resid,
    queries_keys,
    values,
    doc_ids,
    out_weight,
    norm_gain,
    expert_ids,
    gate_vals,
    expert_gate,
    expert_up,
    expert_down,
    shared_gate,
    shared_up,
    shared_down,
    shared_score,
):
    seq_count = lax.axis_size("seq")
    batch_count = lax.axis_size("dp")
    tokens = resid.shape[1]
    model_width = resid.shape[2]
    local_heads = model_width // HD // seq_count
    paired = queries_keys.reshape(2, tokens, seq_count, local_heads, HD)
    valued = values.reshape(1, tokens, seq_count, local_heads, HD)
    documents = doc_ids[0]
    pair_piece = lax.all_to_all(paired, "seq", split_axis=2, concat_axis=1, tiled=True)
    value_piece = lax.all_to_all(valued, "seq", split_axis=2, concat_axis=1, tiled=True)
    attended = attend_heads(
        pair_piece[0, :, 0], pair_piece[1, :, 0], value_piece[0, :, 0], documents
    )
    by_position = attended.reshape(seq_count, tokens, local_heads * HD)
    own_attended = lax.all_to_all(
        by_position, "seq", split_axis=0, concat_axis=2, tiled=True
    ).reshape(tokens, model_width)
    column_block = jnp.dot(
        lax.all_gather(own_attended, "dp", axis=0, tiled=True),
        out_weight,
        preferred_element_type=jnp.float32,
    ).astype(jnp.bfloat16)
    projected = lax.all_to_all(column_block, "dp", split_axis=0, concat_axis=1, tiled=True)
    residual = (resid[0].astype(jnp.float32) + projected.astype(jnp.float32)).astype(jnp.bfloat16)
    stream = residual.astype(jnp.float32)
    normed = (
        stream * lax.rsqrt(jnp.mean(stream * stream, axis=-1, keepdims=True) + norm_eps) * norm_gain
    ).astype(jnp.bfloat16)
    shared_parts = shared_block(
        lax.all_gather(normed, "dp", axis=0, tiled=True), shared_gate, shared_up, shared_down
    )
    shared_sum = lax.psum_scatter(
        shared_parts.astype(jnp.bfloat16), "dp", scatter_dimension=0, tiled=True
    ).astype(jnp.float32)
    share_weight = jax.nn.sigmoid(jnp.dot(normed, shared_score, preferred_element_type=jnp.float32))
    routes = expert_ids[0]
    route_gates = gate_vals[0]
    slot_ids = slot_numbers(routes)
    slot_range = jnp.arange(EXPERTS * CAP, dtype=jnp.int32)
    picked = jnp.sum(
        (slot_ids[None, :, :] == slot_range[:, None, None]).astype(jnp.int32), axis=-1
    ).astype(jnp.bfloat16)
    buffer = jnp.dot(picked, normed, preferred_element_type=jnp.float32).astype(jnp.bfloat16)
    outgoing = jnp.broadcast_to(
        buffer.reshape(EXPERTS, 1, CAP, model_width), (EXPERTS, SPLIT, CAP, model_width)
    )
    own_pieces = expert_gate.shape[0]
    devices = seq_count * batch_count
    incoming = lax.all_to_all(
        outgoing.reshape(EXPERTS * SPLIT, CAP, model_width),
        ("seq", "dp"),
        split_axis=0,
        concat_axis=0,
        tiled=True,
    )
    results = piece_block(
        incoming.reshape(devices, own_pieces, CAP, model_width), expert_gate, expert_up, expert_down
    )
    returned = lax.all_to_all(
        results.reshape(devices * own_pieces, CAP, model_width),
        ("seq", "dp"),
        split_axis=0,
        concat_axis=0,
        tiled=True,
    )
    expert_out = jnp.sum(
        returned.reshape(EXPERTS, SPLIT, CAP, model_width).astype(jnp.float32), axis=1
    ).reshape(EXPERTS * CAP, model_width)
    fetched = jnp.take(expert_out, slot_ids.reshape(-1), axis=0).reshape(tokens, TOPK, model_width)
    routed = jnp.sum(route_gates[..., None] * fetched, axis=1)
    layer_out = residual.astype(jnp.float32) + routed + share_weight[:, None] * shared_sum
    return layer_out.astype(jnp.bfloat16)[None]


def solution(mesh):
    placed = (
        P(("groups", "dp"), "seq", None),
        P(None, ("groups", "dp"), "seq", None),
        P(("groups", "dp"), "seq", None),
        P(("groups", "dp"), None),
        P(None, "dp"),
        P(),
        P(("groups", "dp"), "seq", None),
        P(("groups", "dp"), "seq", None),
        P(("seq", "dp"), None, None),
        P(("seq", "dp"), None, None),
        P(("seq", "dp"), None, None),
        P(None, "dp"),
        P(None, "dp"),
        P("dp", None),
        P(),
    )
    return jax.shard_map(
        body,
        mesh=mesh,
        in_specs=placed,
        out_specs=P(("groups", "dp"), "seq", None),
        check_vma=False,
    )
```

profile of v0, /device:TPU:520, one launch (start us, length us, event | category | flops | bytes accessed | tf_op | source)
XLA Modules:
  0.0 723.0 jit_solution(18105331413996864647)
XLA Ops:
  8.8 13.5 %all-to-all-start = ((bf16[2,64,16,1,128]{4,1,0,3,2:T(8,128)(2,1)}), bf16[2,64,16,1,128]{4,1,0,3,2:T(8,128)(2,1)S(1)}, u32[]{:S(2)}, u32[]{:S(2)}) async-start(bf16[2,64,16,1,128]{4,1,0,3,2:T(8,128)(2,1)} %copy.71), calls=%async_computation | async-start | bytes 1048576 | tf_op jit(solution)/shard_map/all_to_all | solution.py:84
  23.1 14.9 %all-to-all-done = bf16[2,64,16,1,128]{4,1,0,3,2:T(8,128)(2,1)S(1)} async-done(((bf16[2,64,16,1,128]{4,1,0,3,2:T(8,128)(2,1)}), bf16[2,64,16,1,128]{4,1,0,3,2:T(8,128)(2,1)S(1)}, u32[]{:S(2)}, u32[]{:S(2)}) %all-to-all-start) | async-done | bytes 524320 | tf_op jit(solution)/shard_map/all_to_all | solution.py:84
  38.0 4.5 all-to-all-start.1
  46.2 7.5 %all-to-all-done.1 = bf16[1,64,16,1,128]{4,1,3,0,2:T(8,128)(2,1)S(1)} async-done(((bf16[1,64,16,1,128]{4,1,3,0,2:T(8,128)(2,1)}), bf16[1,64,16,1,128]{4,1,3,0,2:T(8,128)(2,1)S(1)}, u32[]{:S(2)}, u32[]{:S(2)}) %all-to-all-start.1) | async-done | bytes 262176 | tf_op jit(solution)/shard_map/all_to_all | solution.py:85
  53.7 3.2 fusion.22
  56.8 14.1 %all_to_all.68 = bf16[16,64,128]{2,1,0:T(8,128)(2,1)S(1)} all-to-all(bf16[16,64,128]{2,1,0:T(8,128)(2,1)S(1)} %bitcast.167), channel_id=1, replica_groups=mesh['groups'=2,'seq'=16,'dp'=8] {'seq'}, dimensions={0} | all-to-all | bytes 524288 | tf_op jit(solution)/shard_map/all_to_all | solution.py:90
  72.8 46.4 %all-gather.3.cloned.1.call-done = bf16[512,2048]{1,0:T(8,128)(2,1)} async-done(((bf16[64,2048]{1,0:T(8,128)(2,1)}), bf16[512,2048]{1,0:T(8,128)(2,1)}) %all-gather.3.cloned.1.call-update) | async-done | bytes 2097168 | tf_op jit(solution)/shard_map/all_gather | solution.py:94
  119.2 3.0 convolution_convert_fusion.3
  122.2 7.4 %all-to-all-start.3 = ((bf16[8,64,256]{2,1,0:T(8,128)(2,1)}), bf16[8,64,256]{2,1,0:T(8,128)(2,1)S(1)}, u32[]{:S(2)}, u32[]{:S(2)}) async-start(bf16[8,64,256]{2,1,0:T(8,128)(2,1)} %bitcast.16), calls=%async_computation.3 | async-start | bytes 524288 | tf_op jit(solution)/shard_map/all_to_all | solution.py:98
  130.3 4.4 all-to-all-done.3
  138.1 2.3 broadcast_in_dim.36
  141.5 247.6 %all_to_all.69 = bf16[128,10,2048]{2,1,0:T(8,128)(2,1)} all-to-all(bf16[128,10,2048]{2,1,0:T(8,128)(2,1)S(1)} %bitcast.156), channel_id=1, replica_groups=mesh['groups'=2,'seq'=16,'dp'=8] {'seq','dp'}, dimensions={0} | all-to-all | bytes 10485760 | tf_op jit(solution)/shard_map/all_to_all | solution.py:124
  389.1 11.9 %fusion.4 = f32[128,10,352]{0,2,1:T(8,128)} fusion(bf16[128,10,2048]{2,1,0:T(8,128)(2,1)} %all_to_all.69, bf16[1,2048,352]{1,2,0:T(8,128)(2,1)S(1)} %copy-done.13), kind=kOutput, calls=%fused_computation.11 | convolution fusion | flops 1845493760 | bytes 8486912 | tf_op jit(solution)/shard_map/npcd,pdf->npcf/dot_general | solution.py:42
  401.1 16.3 %convolution_convert_fusion = bf16[128,10,2048]{2,0,1:T(8,128)(2,1)} fusion(bf16[1,352,2048]{2,1,0:T(8,128)(2,1)S(1)} %copy-done, bf16[1,2048,352]{1,2,0:T(8,128)(2,1)} %param.24, bf16[128,10,2048]{2,1,0:T(8,128)(2,1)} %all_to_all.69, f32[128,10,352]{0,2,1:T(8,128)} %fusion.4), kind=kOutput, calls=%fused_computation.7 | convolution fusion | flops 3696312320 | bytes 15171584 | tf_op jit(solution)/shard_map/npcf,pfd->npcd/dot_general | solution.py:47
  417.4 9.2 %copy.85 = bf16[128,10,2048]{2,1,0:T(8,128)(2,1)} copy(bf16[128,10,2048]{2,0,1:T(8,128)(2,1)} %convolution_convert_fusion) | data formatting | bytes 10485760 | tf_op jit(solution)/shard_map/convert_element_type | solution.py:49
  426.6 12.0 %all-to-all-start.5 = ((bf16[128,10,2048]{2,1,0:T(8,128)(2,1)}), bf16[128,10,2048]{2,1,0:T(8,128)(2,1)}, u32[]{:S(2)}, u32[]{:S(2)}) async-start(bf16[128,10,2048]{2,1,0:T(8,128)(2,1)} %copy.85), calls=%async_computation.5 | async-start | bytes 16777216 | tf_op jit(solution)/shard_map/all_to_all | solution.py:134
  439.5 88.2 %all-gather.5.cloned.1.call-done = bf16[512,2048]{1,0:T(8,128)(2,1)} async-done(((bf16[64,2048]{1,0:T(8,128)(2,1)}), bf16[512,2048]{1,0:T(8,128)(2,1)}) %all-gather.5.cloned.1.call-update) | async-done | bytes 2097168 | tf_op jit(solution)/shard_map/all_gather | solution.py:105
  527.7 3.5 fusion.54
  531.3 5.6 convolution_convert_fusion.1
  538.5 155.8 %all-to-all-done.5 = bf16[128,10,2048]{2,1,0:T(8,128)(2,1)} async-done(((bf16[128,10,2048]{2,1,0:T(8,128)(2,1)}), bf16[128,10,2048]{2,1,0:T(8,128)(2,1)}, u32[]{:S(2)}, u32[]{:S(2)}) %all-to-all-start.5) | async-done | bytes 5242912 | tf_op jit(solution)/shard_map/all_to_all | solution.py:134
  694.3 7.9 %convert_reduce_fusion = f32[32,10,2048]{2,1,0:T(8,128)} fusion(bf16[128,10,2048]{2,1,0:T(8,128)(2,1)} %all-to-all-done.5), kind=kLoop, calls=%fused_computation.1 | loop fusion | flops 4587520 | bytes 7864320 | tf_op jit(solution)/shard_map/reduce_sum | solution.py:141
  702.2 3.2 reshape.181
  705.4 2.7 gather_fusion
  710.1 3.9 multiply_reduce_fusion
  (84 shorter events, 20.2 us)
Async XLA Ops:
  6.5 394.5 %copy-start = (bf16[1,352,2048]{2,1,0:T(8,128)(2,1)S(1)}, bf16[1,352,2048]{2,1,0:T(8,128)(2,1)}, u32[]{:S(2)}) copy-start(bf16[1,352,2048]{2,1,0:T(8,128)(2,1)} %param.25) | copy-start | bytes 4325380
  6.6 15.7 %copy-start.6 = (bf16[1,64,2048]{2,1,0:T(8,128)(2,1)S(1)}, bf16[1,64,2048]{2,1,0:T(8,128)(2,1)}, u32[]{:S(2)}) copy-start(bf16[1,64,2048]{2,1,0:T(8,128)(2,1)} %param.17) | copy-start | bytes 786436
  8.8 29.2 %all-to-all-start = ((bf16[2,64,16,1,128]{4,1,0,3,2:T(8,128)(2,1)}), bf16[2,64,16,1,128]{4,1,0,3,2:T(8,128)(2,1)S(1)}, u32[]{:S(2)}, u32[]{:S(2)}) async-start(bf16[2,64,16,1,128]{4,1,0,3,2:T(8,128)(2,1)} %copy.71), calls=%async_computation | async-start | bytes 1048576 | tf_op jit(solution)/shard_map/all_to_all | solution.py:84
  22.2 20.4 %copy-start.16 = (s32[1,1024]{1,0:T(1,128)S(1)}, s32[1,1024]{1,0:T(1,128)}, u32[]{:S(2)}) copy-start(s32[1,1024]{1,0:T(1,128)} %param.18) | copy-start | bytes 12292
  38.0 15.7 %all-to-all-start.1 = ((bf16[1,64,16,1,128]{4,1,3,0,2:T(8,128)(2,1)}), bf16[1,64,16,1,128]{4,1,3,0,2:T(8,128)(2,1)S(1)}, u32[]{:S(2)}, u32[]{:S(2)}) async-start(bf16[1,64,16,1,128]{4,1,3,0,2:T(8,128)(2,1)} %copy.73), calls=%async_computation.1 | async-start | bytes 524288 | tf_op jit(solution)/shard_map/all_to_all | solution.py:85
  42.4 76.7 %all-gather.3.cloned.1.call-start = ((), (), s32[]{:S(2)}) async-start(), calls=%async_computation.7 | async-start | bytes 2359296 | tf_op jit(solution)/shard_map/all_gather | solution.py:94
  43.6 1.9 copy-start.2
  53.7 18.3 %copy-start.8 = (s32[1,64,4]{1,2,0:T(4,128)S(1)}, s32[1,64,4]{1,2,0:T(4,128)}, u32[]{:S(2)}) copy-start(s32[1,64,4]{1,2,0:T(4,128)} %param.21) | copy-start | bytes 3076
  53.7 65.5 %copy-start.15 = (bf16[2048,256]{1,0:T(8,128)(2,1)S(1)}, bf16[2048,256]{1,0:T(8,128)(2,1)}, u32[]{:S(2)}) copy-start(bf16[2048,256]{1,0:T(8,128)(2,1)} %param.19) | copy-start | bytes 3145732
  122.2 12.6 %copy-start.7 = (bf16[1,64,2048]{2,1,0:T(8,128)(2,1)S(1)}, bf16[1,64,2048]{2,1,0:T(8,128)(2,1)}, u32[]{:S(2)}) copy-start(bf16[1,64,2048]{2,1,0:T(8,128)(2,1)} %param.15) | copy-start | bytes 786436
  122.2 13.5 %copy-start.9 = (f32[2048]{0:T(1024)S(1)}, f32[2048]{0:T(1024)}, u32[]{:S(2)}) copy-start(f32[2048]{0:T(1024)} %param.20) | copy-start | bytes 24580
  122.2 12.5 %all-to-all-start.3 = ((bf16[8,64,256]{2,1,0:T(8,128)(2,1)}), bf16[8,64,256]{2,1,0:T(8,128)(2,1)S(1)}, u32[]{:S(2)}, u32[]{:S(2)}) async-start(bf16[8,64,256]{2,1,0:T(8,128)(2,1)} %bitcast.16), calls=%async_computation.3 | async-start | bytes 524288 | tf_op jit(solution)/shard_map/all_to_all | solution.py:98
  134.9 0.7 copy-start.3
  135.8 0.7 copy-start.4
  141.5 247.7 %copy-start.13 = (bf16[1,2048,352]{1,2,0:T(8,128)(2,1)S(1)}, bf16[1,2048,352]{1,2,0:T(8,128)(2,1)}, u32[]{:S(2)}) copy-start(bf16[1,2048,352]{1,2,0:T(8,128)(2,1)} %param.23) | copy-start | bytes 4325380
  426.6 101.1 %copy-start.14 = (bf16[2048,352]{0,1:T(8,128)(2,1)S(1)}, bf16[2048,352]{0,1:T(8,128)(2,1)}, u32[]{:S(2)}) copy-start(bf16[2048,352]{0,1:T(8,128)(2,1)} %param.26) | copy-start | bytes 4325380
  426.6 267.6 %all-to-all-start.5 = ((bf16[128,10,2048]{2,1,0:T(8,128)(2,1)}), bf16[128,10,2048]{2,1,0:T(8,128)(2,1)}, u32[]{:S(2)}, u32[]{:S(2)}) async-start(bf16[128,10,2048]{2,1,0:T(8,128)(2,1)} %copy.85), calls=%async_computation.5 | async-start | bytes 16777216 | tf_op jit(solution)/shard_map/all_to_all | solution.py:134
  438.6 89.1 %all-gather.5.cloned.1.call-start = ((), (), s32[]{:S(2)}) async-start(), calls=%async_computation.8 | async-start | bytes 2359296 | tf_op jit(solution)/shard_map/all_gather | solution.py:105
  439.4 274.6 %reduce-scatter.2.cloned.1.call-start = ((), (), s32[]{:S(2)}) async-start(), calls=%async_computation.9 | async-start | bytes 2359296 | tf_op jit(solution)/shard_map/reduce_scatter | solution.py:107
  527.7 3.6 copy-start.12
  536.8 0.7 copy-start.11
  536.9 1.4 copy-start.10
  536.9 1.4 copy-start.5
  708.1 7.9 %copy-start.1 = (bf16[1,352,2048]{2,1,0:T(8,128)(2,1)S(1)}, bf16[1,352,2048]{2,1,0:T(8,128)(2,1)}, u32[]{:S(2)}) copy-start(bf16[1,352,2048]{2,1,0:T(8,128)(2,1)} %param.25) | copy-start | bytes 4325380
Sparse Core Ops, SparseCore 0:
  72.1 47.0 all-gather.2
  441.3 86.4 all-gather.4
  537.0 109.4 reduce-scatter.1
where the time goes:
time: 732 us; the launch traced here: 723 us
  waiting for transfers between devices  318 us (43%)
  blocking collectives  262 us (36%)
  matrix products  46.3 us (6%)
  starting transfers between devices  37.4 us (5%)
  local copies, waits for them, and re-layouts  29.9 us (4%)
  other arithmetic  15.7 us (2%)
  between operations  13.9 us (2%)
    all_to_all x1, blocking collectives, body(): lax.all_to_all(outgoing.reshape(EXPERTS * SPLIT, CAP, model_width), ('seq...  248 us
    all_to_all x1, waiting for transfers between devices, body(): lax.all_to_all(results.reshape(devices * own_pieces, CAP, model_width), (...  156 us
    all_gather x1, waiting for transfers between devices, body(): lax.all_gather(normed, 'dp', axis=0, tiled=True)  88.2 us
    all_gather x1, waiting for transfers between devices, body(): lax.all_gather(own_attended, 'dp', axis=0, tiled=True)  46.4 us
    dot_general x1, matrix products, piece_block(): jnp.einsum('npcf,pfd->npcd', hidden, down_matrix, preferred_element_type=...  16.3 us
    all_to_all x1, waiting for transfers between devices, body(): lax.all_to_all(paired, 'seq', split_axis=2, concat_axis=1, tiled=True)  14.9 us
  transfers between devices with their start and end apart: 7, of which 6 were waited for; matrix products, arithmetic and copies ran while one was open for 5% of the time, Pallas kernels for 0%

commit v1 on v0

--- a/solution.py
+++ b/solution.py
@@ -1,3 +1,4 @@
+import functools
 import math
 import jax
 import jax.numpy as jnp
@@ -10,6 +11,35 @@
 SPLIT = 4
 CAP = 10
 norm_eps = 1e-06
+
+
+def supply_rates_now(frame, along_axis):
+    r1, seen_now, fresh = (lax.axis_size(along_axis), lax.axis_index(along_axis), frame.shape[0])
+    gallery = [q * r1 if s == 0 else q for s, q in enumerate(frame.shape)]
+    b_next = lax.dynamic_update_slice_in_dim(
+        jnp.zeros(gallery, frame.dtype), frame, seen_now * fresh, axis=0
+    )
+    f_next = shaped = frame
+    jj = 1
+    while jj < r1 // 2 + 1:
+        f_next = lax.ppermute(
+            f_next, axis_name=along_axis, perm=[(s, (s + 1) % r1) for s in range(r1)]
+        )
+        b_next = lax.dynamic_update_slice_in_dim(
+            b_next, f_next, (seen_now - jj) % r1 * fresh, axis=0
+        )
+        if 2 * jj < r1:
+            shaped = lax.ppermute(
+                shaped, axis_name=along_axis, perm=[(s, (s - 1) % r1) for s in range(r1)]
+            )
+            b_next = lax.dynamic_update_slice_in_dim(
+                b_next, shaped, (seen_now + jj) % r1 * fresh, axis=0
+            )
+        jj = jj + 1
+    return b_next
+
+
+return_all_the_body = functools.partial(supply_rates_now, along_axis="dp")
 
 
 def slot_numbers(routes):
@@ -91,9 +121,7 @@
         by_position, "seq", split_axis=0, concat_axis=2, tiled=True
     ).reshape(tokens, model_width)
     column_block = jnp.dot(
-        lax.all_gather(own_attended, "dp", axis=0, tiled=True),
-        out_weight,
-        preferred_element_type=jnp.float32,
+        return_all_the_body(own_attended), out_weight, preferred_element_type=jnp.float32
     ).astype(jnp.bfloat16)
     projected = lax.all_to_all(column_block, "dp", split_axis=0, concat_axis=1, tiled=True)
     residual = (resid[0].astype(jnp.float32) + projected.astype(jnp.float32)).astype(jnp.bfloat16)

time: 732 us -> 691 us (0.944)
  the two profiles are of different devices: /device:TPU:520 before, /device:TPU:522 now
where the time goes in v1:
time: 691 us; the launch traced here: 682 us
  waiting for transfers between devices  306 us (44%)
  blocking collectives  205 us (30%)
  starting transfers between devices  66 us (10%)
  matrix products  45.5 us (7%)
  local copies, waits for them, and re-layouts  30 us (4%)
  other arithmetic  15.7 us (2%)
  between operations  14.1 us (2%)
    all_to_all x1, blocking collectives, body(): lax.all_to_all(outgoing.reshape(EXPERTS * SPLIT, CAP, model_width), ('seq...  205 us
    all_to_all x1, waiting for transfers between devices, body(): lax.all_to_all(results.reshape(devices * own_pieces, CAP, model_width), (...  154 us
    all_gather x1, waiting for transfers between devices, body(): lax.all_gather(normed, 'dp', axis=0, tiled=True)  91.6 us
    ppermute x4, waiting for transfers between devices, supply_rates_now(): lax.ppermute(f_next, axis_name=along_axis, perm=[(s, (s + 1) % r1) for s...  19.2 us
    all_to_all x1, starting transfers between devices, body(): lax.all_to_all(results.reshape(devices * own_pieces, CAP, model_width), (...  17.9 us
    dot_general x1, matrix products, piece_block(): jnp.einsum('npcf,pfd->npcd', hidden, down_matrix, preferred_element_type=...  16.3 us
    all_to_all x1, waiting for transfers between devices, body(): lax.all_to_all(paired, 'seq', split_axis=2, concat_axis=1, tiled=True)  14.9 us
  transfers between devices with their start and end apart: 14, of which 13 were waited for; matrix products, arithmetic and copies ran while one was open for 5% of the time, Pallas kernels for 0%

profile of v1, /device:TPU:522, one launch (start us, length us, event | category | flops | bytes accessed | tf_op | source)
XLA Modules:
  0.0 681.9 jit_solution(11233820124317710154)
XLA Ops:
  8.8 13.5 %all-to-all-start = ((bf16[2,64,16,1,128]{4,1,0,3,2:T(8,128)(2,1)}), bf16[2,64,16,1,128]{4,1,0,3,2:T(8,128)(2,1)S(1)}, u32[]{:S(2)}, u32[]{:S(2)}) async-start(bf16[2,64,16,1,128]{4,1,0,3,2:T(8,128)(2,1)} %copy.71), calls=%async_computation | async-start | bytes 1048576 | tf_op jit(solution)/shard_map/all_to_all | solution.py:114
  23.1 14.9 %all-to-all-done = bf16[2,64,16,1,128]{4,1,0,3,2:T(8,128)(2,1)S(1)} async-done(((bf16[2,64,16,1,128]{4,1,0,3,2:T(8,128)(2,1)}), bf16[2,64,16,1,128]{4,1,0,3,2:T(8,128)(2,1)S(1)}, u32[]{:S(2)}, u32[]{:S(2)}) %all-to-all-start) | async-done | bytes 524320 | tf_op jit(solution)/shard_map/all_to_all | solution.py:114
  38.0 4.5 all-to-all-start.1
  46.2 7.5 %all-to-all-done.1 = bf16[1,64,16,1,128]{4,1,3,0,2:T(8,128)(2,1)S(1)} async-done(((bf16[1,64,16,1,128]{4,1,3,0,2:T(8,128)(2,1)}), bf16[1,64,16,1,128]{4,1,3,0,2:T(8,128)(2,1)S(1)}, u32[]{:S(2)}, u32[]{:S(2)}) %all-to-all-start.1) | async-done | bytes 262176 | tf_op jit(solution)/shard_map/all_to_all | solution.py:115
  53.7 3.8 fusion.22
  57.4 4.0 all-to-all-start.2
  62.4 9.6 %all-to-all-done.2 = bf16[16,64,128]{2,1,0:T(8,128)(2,1)S(1)} async-done(((bf16[16,64,128]{2,1,0:T(8,128)(2,1)}), bf16[16,64,128]{2,1,0:T(8,128)(2,1)S(1)}, u32[]{:S(2)}, u32[]{:S(2)}) %all-to-all-start.2) | async-done | bytes 262176 | tf_op jit(solution)/shard_map/all_to_all | solution.py:120
  74.7 6.6 collective-permute-done
  83.9 6.5 collective-permute-done.2
  90.4 4.8 collective-permute-start.4
  96.4 4.0 collective-permute-done.4
  109.2 13.7 %all-to-all-start.3 = ((bf16[8,64,256]{2,1,0:T(8,128)(2,1)}), bf16[8,64,256]{2,1,0:T(8,128)(2,1)S(1)}, u32[]{:S(2)}, u32[]{:S(2)}) async-start(bf16[8,64,256]{2,1,0:T(8,128)(2,1)} %bitcast.16), calls=%async_computation.3 | async-start | bytes 524288 | tf_op jit(solution)/shard_map/all_to_all | solution.py:126
  123.6 4.5 all-to-all-done.3
  135.0 205.0 %all_to_all.68 = bf16[128,10,2048]{2,1,0:T(8,128)(2,1)} all-to-all(bf16[128,10,2048]{2,1,0:T(8,128)(2,1)S(1)} %bitcast.158), channel_id=1, replica_groups=mesh['groups'=2,'seq'=16,'dp'=8] {'seq','dp'}, dimensions={0} | all-to-all | bytes 10485760 | tf_op jit(solution)/shard_map/all_to_all | solution.py:152
  340.0 12.1 %fusion.4 = f32[128,10,352]{0,2,1:T(8,128)} fusion(bf16[128,10,2048]{2,1,0:T(8,128)(2,1)} %all_to_all.68, bf16[1,2048,352]{1,2,0:T(8,128)(2,1)S(1)} %copy-done.13), kind=kOutput, calls=%fused_computation.11 | convolution fusion | flops 1845493760 | bytes 8486912 | tf_op jit(solution)/shard_map/npcd,pdf->npcf/dot_general | solution.py:72
  352.1 16.3 %convolution_convert_fusion = bf16[128,10,2048]{2,0,1:T(8,128)(2,1)} fusion(bf16[1,352,2048]{2,1,0:T(8,128)(2,1)S(1)} %copy-done, bf16[1,2048,352]{1,2,0:T(8,128)(2,1)} %param.24, bf16[128,10,2048]{2,1,0:T(8,128)(2,1)} %all_to_all.68, f32[128,10,352]{0,2,1:T(8,128)} %fusion.4), kind=kOutput, calls=%fused_computation.7 | convolution fusion | flops 3696312320 | bytes 15171584 | tf_op jit(solution)/shard_map/npcf,pfd->npcd/dot_general | solution.py:77
  368.5 9.3 %copy.85 = bf16[128,10,2048]{2,1,0:T(8,128)(2,1)} copy(bf16[128,10,2048]{2,0,1:T(8,128)(2,1)} %convolution_convert_fusion) | data formatting | bytes 10485760 | tf_op jit(solution)/shard_map/convert_element_type | solution.py:79
  377.8 17.9 %all-to-all-start.5 = ((bf16[128,10,2048]{2,1,0:T(8,128)(2,1)}), bf16[128,10,2048]{2,1,0:T(8,128)(2,1)}, u32[]{:S(2)}, u32[]{:S(2)}) async-start(bf16[128,10,2048]{2,1,0:T(8,128)(2,1)} %copy.85), calls=%async_computation.5 | async-start | bytes 16777216 | tf_op jit(solution)/shard_map/all_to_all | solution.py:162
  396.6 91.6 %all-gather.2.cloned.1.call-done = bf16[512,2048]{1,0:T(8,128)(2,1)} async-done(((bf16[64,2048]{1,0:T(8,128)(2,1)}), bf16[512,2048]{1,0:T(8,128)(2,1)}) %all-gather.2.cloned.1.call-update) | async-done | bytes 2097168 | tf_op jit(solution)/shard_map/all_gather | solution.py:133
  488.3 3.6 fusion.54
  491.8 5.6 convolution_convert_fusion.1
  499.0 154.0 %all-to-all-done.5 = bf16[128,10,2048]{2,1,0:T(8,128)(2,1)} async-done(((bf16[128,10,2048]{2,1,0:T(8,128)(2,1)}), bf16[128,10,2048]{2,1,0:T(8,128)(2,1)}, u32[]{:S(2)}, u32[]{:S(2)}) %all-to-all-start.5) | async-done | bytes 5242912 | tf_op jit(solution)/shard_map/all_to_all | solution.py:162
  653.0 7.9 %convert_reduce_fusion = f32[32,10,2048]{2,1,0:T(8,128)} fusion(bf16[128,10,2048]{2,1,0:T(8,128)(2,1)} %all-to-all-done.5), kind=kLoop, calls=%fused_computation.1 | loop fusion | flops 4587520 | bytes 7864320 | tf_op jit(solution)/shard_map/reduce_sum | solution.py:169
  669.0 3.9 multiply_reduce_fusion
  (105 shorter events, 42.7 us)
Async XLA Ops:
  6.5 345.6 %copy-start = (bf16[1,352,2048]{2,1,0:T(8,128)(2,1)S(1)}, bf16[1,352,2048]{2,1,0:T(8,128)(2,1)}, u32[]{:S(2)}) copy-start(bf16[1,352,2048]{2,1,0:T(8,128)(2,1)} %param.25) | copy-start | bytes 4325380
  6.6 15.7 %copy-start.6 = (bf16[1,64,2048]{2,1,0:T(8,128)(2,1)S(1)}, bf16[1,64,2048]{2,1,0:T(8,128)(2,1)}, u32[]{:S(2)}) copy-start(bf16[1,64,2048]{2,1,0:T(8,128)(2,1)} %param.17) | copy-start | bytes 786436
  8.8 29.2 %all-to-all-start = ((bf16[2,64,16,1,128]{4,1,0,3,2:T(8,128)(2,1)}), bf16[2,64,16,1,128]{4,1,0,3,2:T(8,128)(2,1)S(1)}, u32[]{:S(2)}, u32[]{:S(2)}) async-start(bf16[2,64,16,1,128]{4,1,0,3,2:T(8,128)(2,1)} %copy.71), calls=%async_computation | async-start | bytes 1048576 | tf_op jit(solution)/shard_map/all_to_all | solution.py:114
  22.2 20.3 %copy-start.16 = (s32[1,1024]{1,0:T(1,128)S(1)}, s32[1,1024]{1,0:T(1,128)}, u32[]{:S(2)}) copy-start(s32[1,1024]{1,0:T(1,128)} %param.18) | copy-start | bytes 12292
  38.0 15.7 %all-to-all-start.1 = ((bf16[1,64,16,1,128]{4,1,3,0,2:T(8,128)(2,1)}), bf16[1,64,16,1,128]{4,1,3,0,2:T(8,128)(2,1)S(1)}, u32[]{:S(2)}, u32[]{:S(2)}) async-start(bf16[1,64,16,1,128]{4,1,3,0,2:T(8,128)(2,1)} %copy.73), calls=%async_computation.1 | async-start | bytes 524288 | tf_op jit(solution)/shard_map/all_to_all | solution.py:115
  53.7 7.9 %copy-start.8 = (s32[1,64,4]{1,2,0:T(4,128)S(1)}, s32[1,64,4]{1,2,0:T(4,128)}, u32[]{:S(2)}) copy-start(s32[1,64,4]{1,2,0:T(4,128)} %param.21) | copy-start | bytes 3076
  57.4 14.6 %all-to-all-start.2 = ((bf16[16,64,128]{2,1,0:T(8,128)(2,1)}), bf16[16,64,128]{2,1,0:T(8,128)(2,1)S(1)}, u32[]{:S(2)}, u32[]{:S(2)}) async-start(bf16[16,64,128]{2,1,0:T(8,128)(2,1)} %bitcast.13), calls=%async_computation.2 | async-start | bytes 524288 | tf_op jit(solution)/shard_map/all_to_all | solution.py:120
  72.3 9.0 %collective-permute-start = (bf16[64,2048]{1,0:T(8,128)(2,1)S(1)}, bf16[64,2048]{1,0:T(8,128)(2,1)S(1)}, u32[]{:S(2)}, u32[]{:S(2)}) collective-permute-start(bf16[64,2048]{1,0:T(8,128)(2,1)S(1)} %bitcast.169), channel_id=1, source_target_pairs={{0,1},{1,2},{2,3},{3,4},{4,5},{5,6},{6,7},{7,0},{8,9},{9,10},{10,1... | collective-permute-start | bytes 786440 | tf_op jit(solution)/shard_map/ppermute | solution.py:25
  73.1 9.2 %collective-permute-start.1 = (bf16[64,2048]{1,0:T(8,128)(2,1)S(1)}, bf16[64,2048]{1,0:T(8,128)(2,1)S(1)}, u32[]{:S(2)}, u32[]{:S(2)}) collective-permute-start(bf16[64,2048]{1,0:T(8,128)(2,1)S(1)} %bitcast.170), channel_id=1, source_target_pairs={{0,7},{1,0},{2,1},{3,2},{4,3},{5,4},{6,5},{7,6},{8,15},{9,8},{10,9... | collective-permute-start | bytes 786440 | tf_op jit(solution)/shard_map/ppermute | solution.py:32
  74.7 33.1 %copy-start.15 = (bf16[2048,256]{1,0:T(8,128)(2,1)S(1)}, bf16[2048,256]{1,0:T(8,128)(2,1)}, u32[]{:S(2)}) copy-start(bf16[2048,256]{1,0:T(8,128)(2,1)} %param.19) | copy-start | bytes 3145732
  81.3 9.1 %collective-permute-start.2 = (bf16[64,2048]{1,0:T(8,128)(2,1)S(1)}, bf16[64,2048]{1,0:T(8,128)(2,1)S(1)}, u32[]{:S(2)}, u32[]{:S(2)}) collective-permute-start(bf16[64,2048]{1,0:T(8,128)(2,1)S(1)} %collective-permute-done), channel_id=1, source_target_pairs={{0,1},{1,2},{2,3},{3,4},{4,5},{5,6},{6,7},{7,0},{8,9},{9,10},{10,1... | collective-permute-start | bytes 786440 | tf_op jit(solution)/shard_map/ppermute | solution.py:25
  82.3 14.1 %collective-permute-start.3 = (bf16[64,2048]{1,0:T(8,128)(2,1)S(1)}, bf16[64,2048]{1,0:T(8,128)(2,1)S(1)}, u32[]{:S(2)}, u32[]{:S(2)}) collective-permute-start(bf16[64,2048]{1,0:T(8,128)(2,1)S(1)} %collective-permute-done.1), channel_id=1, source_target_pairs={{0,7},{1,0},{2,1},{3,2},{4,3},{5,4},{6,5},{7,6},{8,15},{9,8},{10,9... | collective-permute-start | bytes 786440 | tf_op jit(solution)/shard_map/ppermute | solution.py:32
  90.4 10.0 %collective-permute-start.4 = (bf16[64,2048]{1,0:T(8,128)(2,1)S(1)}, bf16[64,2048]{1,0:T(8,128)(2,1)S(1)}, u32[]{:S(2)}, u32[]{:S(2)}) collective-permute-start(bf16[64,2048]{1,0:T(8,128)(2,1)S(1)} %collective-permute-done.2), channel_id=1, source_target_pairs={{0,1},{1,2},{2,3},{3,4},{4,5},{5,6},{6,7},{7,0},{8,9},{9,10},{10,1... | collective-permute-start | bytes 786440 | tf_op jit(solution)/shard_map/ppermute | solution.py:25
  96.4 9.2 %collective-permute-start.5 = (bf16[64,2048]{1,0:T(8,128)(2,1)S(1)}, bf16[64,2048]{1,0:T(8,128)(2,1)S(1)}, u32[]{:S(2)}, u32[]{:S(2)}) collective-permute-start(bf16[64,2048]{1,0:T(8,128)(2,1)S(1)} %collective-permute-done.3), channel_id=1, source_target_pairs={{0,7},{1,0},{2,1},{3,2},{4,3},{5,4},{6,5},{7,6},{8,15},{9,8},{10,9... | collective-permute-start | bytes 786440 | tf_op jit(solution)/shard_map/ppermute | solution.py:32
  100.4 7.3 %collective-permute-start.6 = (bf16[64,2048]{1,0:T(8,128)(2,1)S(1)}, bf16[64,2048]{1,0:T(8,128)(2,1)S(1)}, u32[]{:S(2)}, u32[]{:S(2)}) collective-permute-start(bf16[64,2048]{1,0:T(8,128)(2,1)S(1)} %collective-permute-done.4), channel_id=1, source_target_pairs={{0,1},{1,2},{2,3},{3,4},{4,5},{5,6},{6,7},{7,0},{8,9},{9,10},{10,1... | collective-permute-start | bytes 786440 | tf_op jit(solution)/shard_map/ppermute | solution.py:25
  109.2 19.0 %copy-start.7 = (bf16[1,64,2048]{2,1,0:T(8,128)(2,1)S(1)}, bf16[1,64,2048]{2,1,0:T(8,128)(2,1)}, u32[]{:S(2)}) copy-start(bf16[1,64,2048]{2,1,0:T(8,128)(2,1)} %param.15) | copy-start | bytes 786436
  109.2 19.9 %copy-start.9 = (f32[2048]{0:T(1024)S(1)}, f32[2048]{0:T(1024)}, u32[]{:S(2)}) copy-start(f32[2048]{0:T(1024)} %param.20) | copy-start | bytes 24580
  109.2 19.0 %all-to-all-start.3 = ((bf16[8,64,256]{2,1,0:T(8,128)(2,1)}), bf16[8,64,256]{2,1,0:T(8,128)(2,1)S(1)}, u32[]{:S(2)}, u32[]{:S(2)}) async-start(bf16[8,64,256]{2,1,0:T(8,128)(2,1)} %bitcast.16), calls=%async_computation.3 | async-start | bytes 524288 | tf_op jit(solution)/shard_map/all_to_all | solution.py:126
  135.0 205.0 %copy-start.13 = (bf16[1,2048,352]{1,2,0:T(8,128)(2,1)S(1)}, bf16[1,2048,352]{1,2,0:T(8,128)(2,1)}, u32[]{:S(2)}) copy-start(bf16[1,2048,352]{1,2,0:T(8,128)(2,1)} %param.23) | copy-start | bytes 4325380
  377.8 110.4 %copy-start.14 = (bf16[2048,352]{0,1:T(8,128)(2,1)S(1)}, bf16[2048,352]{0,1:T(8,128)(2,1)}, u32[]{:S(2)}) copy-start(bf16[2048,352]{0,1:T(8,128)(2,1)} %param.26) | copy-start | bytes 4325380
  377.8 275.1 %all-to-all-start.5 = ((bf16[128,10,2048]{2,1,0:T(8,128)(2,1)}), bf16[128,10,2048]{2,1,0:T(8,128)(2,1)}, u32[]{:S(2)}, u32[]{:S(2)}) async-start(bf16[128,10,2048]{2,1,0:T(8,128)(2,1)} %copy.85), calls=%async_computation.5 | async-start | bytes 16777216 | tf_op jit(solution)/shard_map/all_to_all | solution.py:162
  395.8 92.5 %all-gather.2.cloned.1.call-start = ((), (), s32[]{:S(2)}) async-start(), calls=%async_computation.7 | async-start | bytes 2359296 | tf_op jit(solution)/shard_map/all_gather | solution.py:133
  396.6 276.4 %reduce-scatter.2.cloned.1.call-start = ((), (), s32[]{:S(2)}) async-start(), calls=%async_computation.8 | async-start | bytes 2359296 | tf_op jit(solution)/shard_map/reduce_scatter | solution.py:135
  667.0 7.9 %copy-start.1 = (bf16[1,352,2048]{2,1,0:T(8,128)(2,1)S(1)}, bf16[1,352,2048]{2,1,0:T(8,128)(2,1)}, u32[]{:S(2)}) copy-start(bf16[1,352,2048]{2,1,0:T(8,128)(2,1)} %param.25) | copy-start | bytes 4325380
  (7 other events, 10.4 us)
Sparse Core Ops, SparseCore 0:
  398.4 89.8 all-gather.1
  497.6 109.6 reduce-scatter.1
